TPU v7x, 32 devices: a whole 2x2x4 slice. The times are simulated.
32 devices in a mesh: groups: 2 (over y), tensor: 4 (over z), dp: 2 (over x), kv: 2 (over core).
Axes of the slice: x: 2, y: 2, z: 4, core: 2. Of those that a mesh axis runs over, the one named last changes fastest.
Arguments:
- residual: bfloat16 [64, 16384], P(('groups', 'dp'), ('tensor', 'kv')), parts along dimension 0, may hold values from -10 to 10
- query: bfloat16 [64, 8192], P(('groups', 'dp'), ('tensor', 'kv')), parts along dimension 0, may hold values from -60 to 60
- new_pair: bfloat16 [2, 64, 4, 128], P(None, ('groups', 'dp')), parts along dimension 1, may hold values from -8 to 8
- kv_cache: bfloat16 [2, 64, 2048, 4, 128], P(None, ('groups', 'dp'), ('tensor', 'kv')), parts along dimension 1, may hold values from -4.5 to 4.5
- lengths: int32 [64], P(('groups', 'dp')), parts along dimension 0, may hold values from 2 to 2048
- out_weight: bfloat16 [8192, 16384], P(('tensor', 'kv')), may hold values from -0.09375 to 0.09375
- norm_gain: bfloat16 [16384], replicated, may hold values from 0.25 to 1.75
Outputs:
- residual_out: bfloat16 [64, 16384], P(('groups', 'dp'), ('tensor', 'kv')), parts along dimension 0
- mlp_input: bfloat16 [64, 16384], P(('groups', 'dp')), parts along dimension 0
There are 2 independent parts, one for each index of `groups`. A program takes and returns all parts, laid end to end along the dimension named above; an argument that names none is the same for every part. Nothing has to cross between parts.
Inputs may be any that keep to these rules, and one draw needn't show every extreme that they name: Positions below lengths[b] hold sequence b's cache; the others are ignored.
All inputs are finite; a program needn't handle non-finite values.
Results may differ from a plain program's by a relative error of at most 0.007.
Values may be sent and summed in bfloat16 or wider, within the bound.
A program may use at most 128 MiB of HBM per device.

v0:
```python
import math
import jax
import jax.numpy as jnp
from jax import lax
from jax.sharding import PartitionSpec as P

D = 16384
QH = 64
KVH = 4
HD = 128
floor_value = -1e30
epsilon = 1e-05


def on_device(residual, query, new_pair, kv_cache, lengths, out_weight, norm_gain):
    seqs = residual.shape[0]
    width = residual.shape[1]
    per_dev = query.shape[1] // HD
    group = QH // KVH
    scaling = 1.0 / math.sqrt(HD)
    mine = lax.axis_index(("tensor", "kv"))
    queries = lax.all_gather(query, ("tensor", "kv"), axis=1, tiled=True)
    grouped = queries.reshape(seqs, KVH, group, HD)
    span = kv_cache.shape[2]
    places = mine * span + jnp.arange(span, dtype=jnp.int32)
    live = (places[None, :] < lengths[:, None])[:, None, None, :]
    scores = (
        jnp.einsum("bgjd,bpgd->bgjp", grouped, kv_cache[0], preferred_element_type=jnp.float32)
        * scaling
    )
    scores = jnp.where(live, scores, floor_value)
    highest = jnp.max(scores, axis=3)
    weights = jnp.where(live, jnp.exp(scores - highest[..., None]), 0.0)
    totals = jnp.sum(weights, axis=3)
    accum = jnp.einsum("bgjp,bpgd->bgjd", weights, kv_cache[1], preferred_element_type=jnp.float32)
    highest = highest.reshape(seqs, QH)
    totals = totals.reshape(seqs, QH)
    accum = accum.reshape(seqs, QH, HD)
    arrived = (
        lax.all_to_all(highest[None], ("tensor", "kv"), split_axis=2, concat_axis=0, tiled=True),
        lax.all_to_all(totals[None], ("tensor", "kv"), split_axis=2, concat_axis=0, tiled=True),
        lax.all_to_all(accum[None], ("tensor", "kv"), split_axis=2, concat_axis=0, tiled=True),
    )
    best = jnp.max(arrived[0], axis=0)
    factor = jnp.exp(arrived[0] - best[None])
    totals = jnp.sum(arrived[1] * factor, axis=0)
    accum = jnp.sum(arrived[2] * factor[..., None], axis=0)
    highest = best
    own_query = query.reshape(seqs, per_dev, HD).astype(jnp.float32)
    head_ids = mine * per_dev + jnp.arange(per_dev, dtype=jnp.int32)
    selector = (head_ids[:, None] // group == jnp.arange(KVH, dtype=jnp.int32)[None, :]).astype(
        jnp.float32
    )
    fresh_pair = jnp.einsum("hg,sbgd->sbhd", selector, new_pair.astype(jnp.float32))
    fresh = jnp.sum(own_query * fresh_pair[0], axis=2) * scaling
    best = jnp.maximum(highest, fresh)
    old_factor = jnp.exp(highest - best)
    new_factor = jnp.exp(fresh - best)
    totals = totals * old_factor + new_factor
    accum = accum * old_factor[..., None] + new_factor[..., None] * fresh_pair[1]
    attended = (accum / totals[..., None]).astype(jnp.bfloat16).reshape(seqs, per_dev * HD)
    partial_value = jnp.dot(attended, out_weight, preferred_element_type=jnp.float32)
    gain_wide = norm_gain.astype(jnp.float32)
    share = lax.psum_scatter(partial_value, ("tensor", "kv"), scatter_dimension=1, tiled=True)
    stream = (residual.astype(jnp.float32) + share).astype(jnp.bfloat16)
    widened = stream.astype(jnp.float32)
    squares = lax.psum(jnp.sum(widened * widened, axis=1), ("tensor", "kv"))
    gain_mine = lax.dynamic_slice_in_dim(gain_wide, mine * width, width, 0)
    piece = (widened * lax.rsqrt(squares / D + epsilon)[:, None] * gain_mine[None, :]).astype(
        jnp.bfloat16
    )
    normed = lax.all_gather(piece, ("tensor", "kv"), axis=1, tiled=True)
    return (stream, normed)


def solution(mesh):
    placed = (
        P(("groups", "dp"), ("tensor", "kv")),
        P(("groups", "dp"), ("tensor", "kv")),
        P(None, ("groups", "dp"), None, None),
        P(None, ("groups", "dp"), ("tensor", "kv"), None, None),
        P(("groups", "dp")),
        P(("tensor", "kv"), None),
        P(),
    )
    return jax.shard_map(
        on_device,
        mesh=mesh,
        in_specs=placed,
        out_specs=(P(("groups", "dp"), ("tensor", "kv")), P(("groups", "dp"), None)),
        check_vma=False,
    )
```

profile of v0, /device:TPU:0, one launch (start us, length us, event | category | flops | bytes accessed | tf_op | source)
XLA Modules:
  0.0 155.4 jit_solution(17761867516999163748)
XLA Ops:
  7.2 0.0 copy-start
  7.2 0.0 copy-start.2
  7.2 0.0 copy-start.4
  7.2 7.0 %fusion.25 = (bf16[1,16,256,4,128]{4,3,2,1,0:T(4,128)(2,1)}, bf16[1,16,256,4,128]{4,3,2,1,0:T(4,128)(2,1)S(1)}) fusion(bf16[2,16,256,4,128]{4,3,2,1,0:T(4,128)(2,1)} %param.10), kind=kLoop, calls=%fused_computation.48 | loop fusion | bytes 16777216 | tf_op jit(solution)/shard_map/slice | solution.py:35
  14.2 0.0 copy-done.2
  14.2 15.9 %all_gather.6 = bf16[16,8192]{1,0:T(8,128)(2,1)S(1)} all-gather(bf16[16,1024]{1,0:T(8,128)(2,1)S(1)} %copy-done.2), channel_id=1, replica_groups=mesh['groups'=2,'tensor'=4,'dp'=2,'kv'=2] {'tensor','kv'}, dimensions={1}, use_global_device_ids=true | all-gather | bytes 294912 | tf_op jit(solution)/shard_map/all_gather | solution.py:22
  30.2 0.0 copy-done.4
  30.2 0.1 broadcast_compare_fusion
  30.3 1.3 fusion.26
  31.6 0.4 fusion.4
  32.0 0.1 copy.42
  32.1 0.6 broadcast.100
  32.6 0.7 reduce.1
  33.3 0.7 reshape.118
  34.0 4.7 %all-to-all-start.2 = ((f32[8,1,128]{2,1,0:T(1,128)}), f32[8,1,128]{2,1,0:T(1,128)S(1)}, u32[]{:S(2)}, u32[]{:S(2)}) async-start(f32[8,1,128]{2,1,0:T(1,128)} %reshape.118), calls=%async_computation.2 | async-start | bytes 8192 | tf_op jit(solution)/shard_map/all_to_all | solution.py:41
  38.7 0.1 copy.35
  38.8 0.7 reduce.3
  39.5 0.7 reshape.116
  40.2 4.1 %all-to-all-done.2 = f32[8,1,128]{2,1,0:T(1,128)S(1)} async-done(((f32[8,1,128]{2,1,0:T(1,128)}), f32[8,1,128]{2,1,0:T(1,128)S(1)}, u32[]{:S(2)}, u32[]{:S(2)}) %all-to-all-start.2) | async-done | bytes 4128 | tf_op jit(solution)/shard_map/all_to_all | solution.py:41
  44.2 3.3 %all-to-all-start.1 = ((f32[8,1,128]{2,1,0:T(1,128)}), f32[8,1,128]{2,1,0:T(1,128)S(1)}, u32[]{:S(2)}, u32[]{:S(2)}) async-start(f32[8,1,128]{2,1,0:T(1,128)} %reshape.116), calls=%async_computation.1 | async-start | bytes 8192 | tf_op jit(solution)/shard_map/all_to_all | solution.py:40
  47.5 2.9 %fusion = f32[16,4,16,128]{3,2,1,0:T(8,128)S(1)} fusion(bf16[1,16,256,4,128]{4,3,2,1,0:T(4,128)(2,1)} %get-tuple-element.9, f32[16,4,16,256]{3,2,1,0:T(8,128)S(1)} %get-tuple-element.12, f32[16,4,16]{2,1,0:T(4,128)S(1)} %get-tuple-element.11, pred[16,256]{1,0:T(8,128)(4,1)S(1)} %broadcast_compare_fusion), kind=kOutput, calls=%fused_computation.1 | convolution fusion | flops 67633152 | bytes 5775360 | tf_op jit(solution)/shard_map/bgjp,bpgd->bgjd/dot_general | solution.py:35
  50.4 1.1 copy.34
  51.5 1.5 all-to-all-done.1
  53.0 3.5 %all-to-all-start = ((f32[1,16,64,128]{3,1,0,2:T(8,128)}), f32[1,16,64,128]{3,1,0,2:T(8,128)S(1)}, u32[]{:S(2)}, u32[]{:S(2)}) async-start(f32[1,16,64,128]{3,1,0,2:T(8,128)} %copy.34), calls=%async_computation | async-start | bytes 1048576 | tf_op jit(solution)/shard_map/all_to_all | solution.py:42
  56.5 0.0 reduce-scatter.2.cloned.1.call-start
  56.6 0.0 copy-done
  56.6 0.2 convolution_bitcast_fusion
  56.9 0.1 fusion.14
  57.0 0.1 copy.36
  57.0 0.6 reduce.2
  57.7 0.1 reshape.119
  57.8 0.6 reduce.4
  58.4 0.1 reshape.117
  58.6 0.1 copy.38
  58.6 0.1 copy.40
  58.7 13.1 %all-to-all-done = f32[1,16,64,128]{3,1,0,2:T(8,128)S(1)} async-done(((f32[1,16,64,128]{3,1,0,2:T(8,128)}), f32[1,16,64,128]{3,1,0,2:T(8,128)S(1)}, u32[]{:S(2)}, u32[]{:S(2)}) %all-to-all-start) | async-done | bytes 524320 | tf_op jit(solution)/shard_map/all_to_all | solution.py:42
  71.9 0.2 multiply_reduce_fusion
  72.1 0.1 mul.110
  72.1 0.1 div.30
  72.2 0.0 copy-start.3
  72.2 13.9 %fusion.15 = f32[16,16384]{1,0:T(8,128)} fusion(bf16[1024,16384]{1,0:T(8,128)(2,1)} %param.12, f32[2,8,8,128]{3,2,1,0:T(8,128)S(1)} %bitcast.90, f32[2,8,8,128]{3,2,1,0:T(8,128)S(1)} %bitcast.88, f32[2,8,8,128]{3,2,1,0:T(8,128)S(1)} %bitcast.89, f32[16,8,128]{2,0,1:T(8,128)S(1)} %multiply_reduce_fusion, f32[16,8]{0,1:T(8,128)S(1)} %get-tuple-element.5), kind=kOutput, calls=%fused_computation.28 | convolution fusion | flops 536952832 | bytes 34865664 | tf_op jit(solution)/shard_map/dot_general | solution.py:62
  86.2 0.0 reduce-scatter.2.cloned.1.call-update
  86.2 0.7 dynamic-slice_convert_fusion
  86.9 31.0 %reduce-scatter.2.cloned.1.call-done = f32[16,2048]{1,0:T(8,128)} async-done(((f32[16,16384]{1,0:T(8,128)}), f32[16,2048]{1,0:T(8,128)}) %reduce-scatter.2.cloned.1.call-update) | async-done | bytes 131088 | tf_op jit(solution)/shard_map/reduce_scatter | solution.py:64
  117.9 0.0 copy-done.3
  117.9 1.0 fusion.8
  118.9 0.0 copy-start.1
  118.9 13.8 %psum.7 = f32[16]{0:T(128)S(1)} all-reduce(f32[16]{0:T(128)S(1)} %get-tuple-element.2), channel_id=1, replica_groups=mesh['groups'=2,'tensor'=4,'dp'=2,'kv'=2] {'tensor','kv'}, use_global_device_ids=true, to_apply=%region_8.9 | all-reduce | flops 16 | bytes 128 | tf_op jit(solution)/shard_map/psum | solution.py:67
  132.8 0.1 fusion.10
  132.9 14.9 %all_gather.7 = bf16[16,16384]{1,0:T(8,128)(2,1)S(1)} all-gather(bf16[16,2048]{1,0:T(8,128)(2,1)S(1)} %fusion.10), channel_id=1, replica_groups=mesh['groups'=2,'tensor'=4,'dp'=2,'kv'=2] {'tensor','kv'}, dimensions={1}, use_global_device_ids=true | all-gather | bytes 589824 | tf_op jit(solution)/shard_map/all_gather | solution.py:72
  147.8 0.8 copy.70
  148.6 0.0 copy-done.1
  (10 shorter events, 0.1 us)
Async XLA Ops:
  7.2 49.5 %copy-start = (bf16[2,16,4,128]{3,2,1,0:T(4,128)(2,1)S(1)}, bf16[2,16,4,128]{3,2,1,0:T(4,128)(2,1)}, u32[]{:S(2)}) copy-start(bf16[2,16,4,128]{3,2,1,0:T(4,128)(2,1)} %param.9) | copy-start | bytes 98308
  7.2 7.0 %copy-start.2 = (bf16[16,1024]{1,0:T(8,128)(2,1)S(1)}, bf16[16,1024]{1,0:T(8,128)(2,1)}, u32[]{:S(2)}) copy-start(bf16[16,1024]{1,0:T(8,128)(2,1)} %param.8) | copy-start | bytes 98308
  7.2 23.0 %copy-start.4 = (s32[16]{0:T(128)S(1)}, s32[16]{0:T(128)}, u32[]{:S(2)}) copy-start(s32[16]{0:T(128)} %param.11) | copy-start | bytes 196
  34.0 10.2 %all-to-all-start.2 = ((f32[8,1,128]{2,1,0:T(1,128)}), f32[8,1,128]{2,1,0:T(1,128)S(1)}, u32[]{:S(2)}, u32[]{:S(2)}) async-start(f32[8,1,128]{2,1,0:T(1,128)} %reshape.118), calls=%async_computation.2 | async-start | bytes 8192 | tf_op jit(solution)/shard_map/all_to_all | solution.py:41
  44.2 8.8 %all-to-all-start.1 = ((f32[8,1,128]{2,1,0:T(1,128)}), f32[8,1,128]{2,1,0:T(1,128)S(1)}, u32[]{:S(2)}, u32[]{:S(2)}) async-start(f32[8,1,128]{2,1,0:T(1,128)} %reshape.116), calls=%async_computation.1 | async-start | bytes 8192 | tf_op jit(solution)/shard_map/all_to_all | solution.py:40
  53.0 18.9 %all-to-all-start = ((f32[1,16,64,128]{3,1,0,2:T(8,128)}), f32[1,16,64,128]{3,1,0,2:T(8,128)S(1)}, u32[]{:S(2)}, u32[]{:S(2)}) async-start(f32[1,16,64,128]{3,1,0,2:T(8,128)} %copy.34), calls=%async_computation | async-start | bytes 1048576 | tf_op jit(solution)/shard_map/all_to_all | solution.py:42
  56.5 61.3 %reduce-scatter.2.cloned.1.call-start = ((), (), s32[]{:S(2)}) async-start(), calls=%async_computation.4 | async-start | bytes 1179648 | tf_op jit(solution)/shard_map/reduce_scatter | solution.py:64
  72.2 45.7 %copy-start.3 = (bf16[16,2048]{1,0:T(8,128)(2,1)S(1)}, bf16[16,2048]{1,0:T(8,128)(2,1)}, u32[]{:S(2)}) copy-start(bf16[16,2048]{1,0:T(8,128)(2,1)} %param.7) | copy-start | bytes 196612
  118.9 29.7 %copy-start.1 = (bf16[16,2048]{1,0:T(8,128)(2,1)}, bf16[16,2048]{1,0:T(8,128)(2,1)S(1)}, u32[]{:S(2)}) copy-start(bf16[16,2048]{1,0:T(8,128)(2,1)S(1)} %get-tuple-element.15) | copy-start | bytes 196612
Sparse Core Ops, SparseCore 0:
  86.3 31.5 reduce-scatter.1
where the time goes:
time: 156 us; the launch traced here: 155 us
  waiting for transfers between devices  49.7 us (32%)
  blocking collectives  44.7 us (29%)
  matrix products  18.3 us (12%)
  between operations  14.2 us (9%)
  local copies, waits for them, and re-layouts  11.7 us (8%)
  starting transfers between devices  11.5 us (7%)
  other arithmetic  5.32 us (3%)
    reduce_scatter x1, waiting for transfers between devices, on_device(): lax.psum_scatter(partial_value, ('tensor', 'kv'), scatter_dimension=1, ti...  31 us
    all_gather x1, blocking collectives, on_device(): queries = lax.all_gather(query, ('tensor', 'kv'), axis=1, tiled=True)  15.9 us
    all_gather x1, blocking collectives, on_device(): normed = lax.all_gather(piece, ('tensor', 'kv'), axis=1, tiled=True)  14.9 us
    dot_general x1, matrix products, on_device(): jnp.dot(attended, out_weight, preferred_element_type=jnp.float32)  13.9 us
    psum x1, blocking collectives, on_device(): squares = lax.psum(jnp.sum(widened * widened, axis=1), ('tensor', 'kv'))  13.8 us
    all_to_all x1, waiting for transfers between devices, on_device(): lax.all_to_all(accum[None], ('tensor', 'kv'), split_axis=2, concat_axis=0...  13.1 us
    slice x1, local copies, waits for them, and re-layouts, on_device(): kv_cache[1]  7.01 us
    all_to_all x1, starting transfers between devices, on_device(): lax.all_to_all(totals[None], ('tensor', 'kv'), split_axis=2, concat_axis=...  4.68 us
  transfers between devices with their start and end apart: 4, of which 4 were waited for; matrix products, arithmetic and copies ran while one was open for 5% of the time, Pallas kernels for 0%

commit v1 on v0

--- a/solution.py
+++ b/solution.py
@@ -19,7 +19,8 @@
     group = QH // KVH
     scaling = 1.0 / math.sqrt(HD)
     mine = lax.axis_index(("tensor", "kv"))
-    queries = lax.all_gather(query, ("tensor", "kv"), axis=1, tiled=True)
+    blocks = lax.all_gather(query, ("tensor", "kv"))
+    queries = jnp.concatenate(blocks, axis=1)
     grouped = queries.reshape(seqs, KVH, group, HD)
     span = kv_cache.shape[2]
     places = mine * span + jnp.arange(span, dtype=jnp.int32)

time: 156 us -> 159 us (1.019)
  matrix products: 18.3 us -> 20.5 us
    dot_general x1, matrix products: 1.3 us -> 3.48 us  [on_device(): jnp.einsum('bgjd,bpgd->bgjp', grouped, kv_cache[0], preferred_element_typ...]
where the time goes in v1:
time: 159 us
  waiting for transfers between devices  49.7 us (31%)
  blocking collectives  44.7 us (28%)
  matrix products  20.5 us (13%)
  between operations  14.2 us (9%)
  local copies, waits for them, and re-layouts  13 us (8%)
  starting transfers between devices  11.5 us (7%)
  other arithmetic  5.31 us (3%)
    reduce_scatter x1, waiting for transfers between devices, on_device(): lax.psum_scatter(partial_value, ('tensor', 'kv'), scatter_dimension=1, ti...  31 us
    all_gather x1, blocking collectives, on_device(): blocks = lax.all_gather(query, ('tensor', 'kv'))  15.9 us
    all_gather x1, blocking collectives, on_device(): normed = lax.all_gather(piece, ('tensor', 'kv'), axis=1, tiled=True)  14.9 us
    dot_general x1, matrix products, on_device(): jnp.dot(attended, out_weight, preferred_element_type=jnp.float32)  13.9 us
    psum x1, blocking collectives, on_device(): squares = lax.psum(jnp.sum(widened * widened, axis=1), ('tensor', 'kv'))  13.8 us
    all_to_all x1, waiting for transfers between devices, on_device(): lax.all_to_all(accum[None], ('tensor', 'kv'), split_axis=2, concat_axis=0...  13.1 us
    slice x1, local copies, waits for them, and re-layouts, on_device(): kv_cache[1]  8.09 us
    all_to_all x1, starting transfers between devices, on_device(): lax.all_to_all(totals[None], ('tensor', 'kv'), split_axis=2, concat_axis=...  4.68 us
  transfers between devices with their start and end apart: 4, of which 4 were waited for; matrix products, arithmetic and copies ran while one was open for 5% of the time, Pallas kernels for 0%

profile of v1, /device:TPU:0, one launch (start us, length us, event | category | flops | bytes accessed | tf_op | source)
XLA Modules:
  0.0 158.9 jit_solution(16165509183633040035)
XLA Ops:
  7.2 0.0 copy-start
  7.2 0.0 copy-start.2
  7.2 0.0 copy-start.4
  7.2 8.1 %fusion.25 = (bf16[1,16,256,4,128]{4,3,2,1,0:T(4,128)(2,1)}, bf16[1,16,256,4,128]{4,3,2,1,0:T(4,128)(2,1)}) fusion(bf16[2,16,256,4,128]{4,3,2,1,0:T(4,128)(2,1)} %param.10), kind=kLoop, calls=%fused_computation.49 | loop fusion | bytes 16777216 | tf_op jit(solution)/shard_map/slice | solution.py:36
  15.3 0.0 copy-done.2
  15.3 15.9 %all-gather = bf16[128,1024]{1,0:T(8,128)(2,1)S(1)} all-gather(bf16[16,1024]{1,0:T(8,128)(2,1)S(1)} %copy-done.2), channel_id=2, replica_groups=mesh['groups'=2,'tensor'=4,'dp'=2,'kv'=2] {'tensor','kv'}, dimensions={0}, use_global_device_ids=true | all-gather | bytes 294912 | tf_op jit(solution)/shard_map/all_gather | solution.py:22
  31.2 0.1 copy.74
  31.4 0.1 reshape_reshape.3
  31.5 0.0 copy-done.4
  31.5 0.1 broadcast_compare_fusion
  31.6 3.5 %fusion.26 = (f32[16,4,16]{2,1,0:T(4,128)S(1)}, f32[16,4,16,256]{3,2,1,0:T(8,128)S(1)}) fusion(bf16[16,4,16,128]{3,2,1,0:T(8,128)(2,1)S(1)} %reshape_reshape.3, bf16[1,16,256,4,128]{4,3,2,1,0:T(4,128)(2,1)} %get-tuple-element.10, pred[16,256]{1,0:T(8,128)(4,1)S(1)} %broadcast_compare_fusion), kind=kOutput, calls=%fused_computation.50 | convolution fusion | flops 67894272 | bytes 5513216 | tf_op jit(solution)/shard_map/bgjd,bpgd->bgjp/dot_general | solution.py:29
  35.1 0.4 fusion.4
  35.5 0.1 copy.47
  35.6 0.6 broadcast.100
  36.1 0.7 reduce.1
  36.8 0.7 reshape.119
  37.5 4.7 %all-to-all-start.2 = ((f32[8,1,128]{2,1,0:T(1,128)}), f32[8,1,128]{2,1,0:T(1,128)S(1)}, u32[]{:S(2)}, u32[]{:S(2)}) async-start(f32[8,1,128]{2,1,0:T(1,128)} %reshape.119), calls=%async_computation.2 | async-start | bytes 8192 | tf_op jit(solution)/shard_map/all_to_all | solution.py:42
  42.2 0.1 copy.40
  42.3 0.7 reduce.3
  43.0 0.7 reshape.117
  43.6 4.1 %all-to-all-done.2 = f32[8,1,128]{2,1,0:T(1,128)S(1)} async-done(((f32[8,1,128]{2,1,0:T(1,128)}), f32[8,1,128]{2,1,0:T(1,128)S(1)}, u32[]{:S(2)}, u32[]{:S(2)}) %all-to-all-start.2) | async-done | bytes 4128 | tf_op jit(solution)/shard_map/all_to_all | solution.py:42
  47.7 3.3 %all-to-all-start.1 = ((f32[8,1,128]{2,1,0:T(1,128)}), f32[8,1,128]{2,1,0:T(1,128)S(1)}, u32[]{:S(2)}, u32[]{:S(2)}) async-start(f32[8,1,128]{2,1,0:T(1,128)} %reshape.117), calls=%async_computation.1 | async-start | bytes 8192 | tf_op jit(solution)/shard_map/all_to_all | solution.py:41
  51.0 2.9 %fusion = f32[16,4,16,128]{3,2,1,0:T(8,128)S(1)} fusion(bf16[1,16,256,4,128]{4,3,2,1,0:T(4,128)(2,1)} %get-tuple-element.9, f32[16,4,16,256]{3,2,1,0:T(8,128)S(1)} %get-tuple-element.12, f32[16,4,16]{2,1,0:T(4,128)S(1)} %get-tuple-element.11, pred[16,256]{1,0:T(8,128)(4,1)S(1)} %broadcast_compare_fusion), kind=kOutput, calls=%fused_computation.1 | convolution fusion | flops 67633152 | bytes 5775360 | tf_op jit(solution)/shard_map/bgjp,bpgd->bgjd/dot_general | solution.py:36
  53.9 1.1 copy.39
  55.0 1.5 all-to-all-done.1
  56.5 3.5 %all-to-all-start = ((f32[1,16,64,128]{3,1,0,2:T(8,128)}), f32[1,16,64,128]{3,1,0,2:T(8,128)S(1)}, u32[]{:S(2)}, u32[]{:S(2)}) async-start(f32[1,16,64,128]{3,1,0,2:T(8,128)} %copy.39), calls=%async_computation | async-start | bytes 1048576 | tf_op jit(solution)/shard_map/all_to_all | solution.py:43
  60.0 0.0 reduce-scatter.2.cloned.1.call-start
  60.1 0.0 copy-done
  60.1 0.2 convolution_bitcast_fusion
  60.3 0.1 fusion.14
  60.4 0.1 copy.41
  60.5 0.6 reduce.2
  61.1 0.1 reshape.120
  61.2 0.6 reduce.4
  61.9 0.1 reshape.118
  62.0 0.1 copy.43
  62.1 0.1 copy.45
  62.2 13.1 %all-to-all-done = f32[1,16,64,128]{3,1,0,2:T(8,128)S(1)} async-done(((f32[1,16,64,128]{3,1,0,2:T(8,128)}), f32[1,16,64,128]{3,1,0,2:T(8,128)S(1)}, u32[]{:S(2)}, u32[]{:S(2)}) %all-to-all-start) | async-done | bytes 524320 | tf_op jit(solution)/shard_map/all_to_all | solution.py:43
  75.3 0.2 multiply_reduce_fusion
  75.5 0.1 mul.110
  75.6 0.1 div.30
  75.7 0.0 copy-start.3
  75.7 13.9 %fusion.15 = f32[16,16384]{1,0:T(8,128)} fusion(bf16[1024,16384]{1,0:T(8,128)(2,1)} %param.12, f32[2,8,8,128]{3,2,1,0:T(8,128)S(1)} %bitcast.91, f32[2,8,8,128]{3,2,1,0:T(8,128)S(1)} %bitcast.89, f32[2,8,8,128]{3,2,1,0:T(8,128)S(1)} %bitcast.90, f32[16,8,128]{2,0,1:T(8,128)S(1)} %multiply_reduce_fusion, f32[16,8]{0,1:T(8,128)S(1)} %get-tuple-element.5), kind=kOutput, calls=%fused_computation.29 | convolution fusion | flops 536952832 | bytes 34865664 | tf_op jit(solution)/shard_map/dot_general | solution.py:63
  89.6 0.0 reduce-scatter.2.cloned.1.call-update
  89.7 0.7 dynamic-slice_convert_fusion
  90.4 31.0 %reduce-scatter.2.cloned.1.call-done = f32[16,2048]{1,0:T(8,128)} async-done(((f32[16,16384]{1,0:T(8,128)}), f32[16,2048]{1,0:T(8,128)}) %reduce-scatter.2.cloned.1.call-update) | async-done | bytes 131088 | tf_op jit(solution)/shard_map/reduce_scatter | solution.py:65
  121.3 0.0 copy-done.3
  121.4 1.0 fusion.8
  122.4 0.0 copy-start.1
  122.4 13.8 %psum.7 = f32[16]{0:T(128)S(1)} all-reduce(f32[16]{0:T(128)S(1)} %get-tuple-element.2), channel_id=1, replica_groups=mesh['groups'=2,'tensor'=4,'dp'=2,'kv'=2] {'tensor','kv'}, use_global_device_ids=true, to_apply=%region_8.9 | all-reduce | flops 16 | bytes 128 | tf_op jit(solution)/shard_map/psum | solution.py:68
  136.2 0.1 fusion.10
  136.3 14.9 %all_gather.11 = bf16[16,16384]{1,0:T(8,128)(2,1)S(1)} all-gather(bf16[16,2048]{1,0:T(8,128)(2,1)S(1)} %fusion.10), channel_id=1, replica_groups=mesh['groups'=2,'tensor'=4,'dp'=2,'kv'=2] {'tensor','kv'}, dimensions={1}, use_global_device_ids=true | all-gather | bytes 589824 | tf_op jit(solution)/shard_map/all_gather | solution.py:73
  151.3 0.8 copy.76
  152.1 0.0 copy-done.1
  (9 shorter events, 0.1 us)
Async XLA Ops:
  7.2 52.9 %copy-start = (bf16[2,16,4,128]{3,2,1,0:T(4,128)(2,1)S(1)}, bf16[2,16,4,128]{3,2,1,0:T(4,128)(2,1)}, u32[]{:S(2)}) copy-start(bf16[2,16,4,128]{3,2,1,0:T(4,128)(2,1)} %param.9) | copy-start | bytes 98308
  7.2 8.1 %copy-start.2 = (bf16[16,1024]{1,0:T(8,128)(2,1)S(1)}, bf16[16,1024]{1,0:T(8,128)(2,1)}, u32[]{:S(2)}) copy-start(bf16[16,1024]{1,0:T(8,128)(2,1)} %param.8) | copy-start | bytes 98308
  7.2 24.3 %copy-start.4 = (s32[16]{0:T(128)S(1)}, s32[16]{0:T(128)}, u32[]{:S(2)}) copy-start(s32[16]{0:T(128)} %param.11) | copy-start | bytes 196
  37.5 10.2 %all-to-all-start.2 = ((f32[8,1,128]{2,1,0:T(1,128)}), f32[8,1,128]{2,1,0:T(1,128)S(1)}, u32[]{:S(2)}, u32[]{:S(2)}) async-start(f32[8,1,128]{2,1,0:T(1,128)} %reshape.119), calls=%async_computation.2 | async-start | bytes 8192 | tf_op jit(solution)/shard_map/all_to_all | solution.py:42
  47.7 8.8 %all-to-all-start.1 = ((f32[8,1,128]{2,1,0:T(1,128)}), f32[8,1,128]{2,1,0:T(1,128)S(1)}, u32[]{:S(2)}, u32[]{:S(2)}) async-start(f32[8,1,128]{2,1,0:T(1,128)} %reshape.117), calls=%async_computation.1 | async-start | bytes 8192 | tf_op jit(solution)/shard_map/all_to_all | solution.py:41
  56.5 18.9 %all-to-all-start = ((f32[1,16,64,128]{3,1,0,2:T(8,128)}), f32[1,16,64,128]{3,1,0,2:T(8,128)S(1)}, u32[]{:S(2)}, u32[]{:S(2)}) async-start(f32[1,16,64,128]{3,1,0,2:T(8,128)} %copy.39), calls=%async_computation | async-start | bytes 1048576 | tf_op jit(solution)/shard_map/all_to_all | solution.py:43
  60.0 61.3 %reduce-scatter.2.cloned.1.call-start = ((), (), s32[]{:S(2)}) async-start(), calls=%async_computation.4 | async-start | bytes 1179648 | tf_op jit(solution)/shard_map/reduce_scatter | solution.py:65
  75.7 45.7 %copy-start.3 = (bf16[16,2048]{1,0:T(8,128)(2,1)S(1)}, bf16[16,2048]{1,0:T(8,128)(2,1)}, u32[]{:S(2)}) copy-start(bf16[16,2048]{1,0:T(8,128)(2,1)} %param.7) | copy-start | bytes 196612
  122.4 29.7 %copy-start.1 = (bf16[16,2048]{1,0:T(8,128)(2,1)}, bf16[16,2048]{1,0:T(8,128)(2,1)S(1)}, u32[]{:S(2)}) copy-start(bf16[16,2048]{1,0:T(8,128)(2,1)S(1)} %get-tuple-element.15) | copy-start | bytes 196612
Sparse Core Ops, SparseCore 0:
  89.8 31.5 reduce-scatter.1
